TPU v7x, 32 devices: a whole 2x2x4 slice. The times are simulated.
32 devices in a mesh: pr: 8 (over y, x, core), pc: 4 (over z).
Axes of the slice: x: 2, y: 2, z: 4, core: 2. Of those that a mesh axis runs over, the one named last changes fastest.
Arguments:
- pair_array: bfloat16 [256, 256, 128], P('pr', 'pc'), may hold values from -6 to 6
- left_weight: bfloat16 [128, 128], replicated, may hold values from -0.5 to 0.5
- right_weight: bfloat16 [128, 128], replicated, may hold values from -0.5 to 0.5
- left_gate: bfloat16 [128, 128], replicated, may hold values from -0.5 to 0.5
- right_gate: bfloat16 [128, 128], replicated, may hold values from -0.5 to 0.5
- mid_gain: float32 [128], replicated, may hold values from 0.25 to 1.75
- out_weight: bfloat16 [128, 128], replicated, may hold values from -0.5 to 0.5
- out_gate: bfloat16 [128, 128], replicated, may hold values from -0.5 to 0.5
Outputs:
- pair_update: bfloat16 [256, 256, 128], P('pr', 'pc')
All inputs are finite; a program needn't handle non-finite values.
Results may differ from a plain program's by a relative error of at most 0.012.
Values may be sent and summed in bfloat16 or wider, within the bound.
A program may use at most 128 MiB of HBM per device.

v0:
```python
import jax
import jax.numpy as jnp
from jax import lax
from jax.sharding import PartitionSpec as P


def unit_channels(values, channel_gain):
    centred = values - jnp.mean(values, axis=-1, keepdims=True)
    return (
        centred
        * lax.rsqrt(jnp.mean(centred * centred, axis=-1, keepdims=True) + 1e-05)
        * channel_gain
    )


def make_factors(pair_in, left_weight, right_weight, left_gate, right_gate):
    left = jnp.einsum("ijc,cd->ijd", pair_in, left_weight, preferred_element_type=jnp.float32)
    left = left * jax.nn.sigmoid(
        jnp.einsum("ijc,cd->ijd", pair_in, left_gate, preferred_element_type=jnp.float32)
    )
    right = jnp.einsum("ijc,cd->ijd", pair_in, right_weight, preferred_element_type=jnp.float32)
    right = right * jax.nn.sigmoid(
        jnp.einsum("ijc,cd->ijd", pair_in, right_gate, preferred_element_type=jnp.float32)
    )
    return (pair_in, left.astype(jnp.bfloat16), right.astype(jnp.bfloat16))


def to_pair(mixed, ready, mid_gain, out_weight, out_gate):
    scaled = unit_channels(mixed.astype(jnp.float32), mid_gain).astype(jnp.bfloat16)
    scaled = lax.optimization_barrier(scaled)
    gate = jax.nn.sigmoid(
        jnp.einsum("ijc,cd->ijd", ready, out_gate, preferred_element_type=jnp.float32)
    )
    return (
        jnp.einsum("ijd,dc->ijc", scaled, out_weight, preferred_element_type=jnp.float32) * gate
    ).astype(jnp.bfloat16)


def on_device(
    pair_array, left_weight, right_weight, left_gate, right_gate, mid_gain, out_weight, out_gate
):
    ready, left, right = make_factors(pair_array, left_weight, right_weight, left_gate, right_gate)
    count = pair_array.shape[0] * lax.axis_size("pr")
    left_lines, right_lines = (
        lax.all_to_all(left, "pr", split_axis=2, concat_axis=0, tiled=True),
        lax.all_to_all(right, "pr", split_axis=2, concat_axis=0, tiled=True),
    )
    strip = jnp.einsum(
        "kid,kjd->ijd",
        lax.all_gather(left_lines, "pc", axis=1, tiled=True),
        right_lines,
        preferred_element_type=jnp.float32,
    )
    strip = (strip * count ** (-0.5)).astype(jnp.bfloat16)
    mixed = lax.all_to_all(strip, "pr", split_axis=0, concat_axis=2, tiled=True)
    return to_pair(mixed, ready, mid_gain, out_weight, out_gate)


def solution(mesh):
    return jax.shard_map(
        on_device,
        mesh=mesh,
        in_specs=(P("pr", "pc", None), P(), P(), P(), P(), P(), P(), P()),
        out_specs=P("pr", "pc", None),
        check_vma=False,
    )
```

profile of v0, /device:TPU:0, one launch (start us, length us, event | category | flops | bytes accessed | tf_op | source)
XLA Modules:
  0.0 104.0 jit_solution(1541400130074911763)
XLA Ops:
  6.5 1.0 copy-done
  7.6 1.0 fusion.24
  8.6 1.2 %fusion.14 = bf16[32,64,128]{2,1,0:T(8,128)(2,1)S(1)} fusion(f32[32,64,128]{2,1,0:T(8,128)S(1)} %fusion.24, bf16[32,64,128]{2,1,0:T(8,128)(2,1)S(1)} %copy-done, bf16[128,128]{1,0:T(8,128)(2,1)} %param.11), kind=kOutput, calls=%fused_computation.22 | convolution fusion | flops 68419584 | bytes 2129920 | tf_op jit(solution)/shard_map/ijc,cd->ijd/dot_general | solution.py:19
  9.8 1.6 %copy.25 = bf16[32,64,128]{1,0,2:T(8,128)(2,1)S(1)} copy(bf16[32,64,128]{2,1,0:T(8,128)(2,1)S(1)} %fusion.14) | data formatting | bytes 1048576 | tf_op jit(solution)/shard_map/convert_element_type | solution.py:25
  11.4 0.7 reshape.28
  12.2 14.7 %all_to_all.45 = bf16[8,2,16384]{2,1,0:T(2,128)(2,1)S(1)} all-to-all(bf16[8,2,16384]{2,1,0:T(2,128)(2,1)S(1)} %reshape.28), channel_id=1, replica_groups=mesh['pr'=8,'pc'=4] {'pr'}, dimensions={0} | all-to-all | bytes 1048576 | tf_op jit(solution)/shard_map/all_to_all | solution.py:45
  26.8 0.7 reshape.29
  27.5 0.4 copy.27
  28.0 1.6 %copy.28 = bf16[256,64,16]{0,1,2:T(8,128)(2,1)} copy(bf16[256,64,16]{1,2,0:T(8,128)(2,1)S(1)} %bitcast.66) | data formatting | bytes 1048576 | tf_op jit(solution)/shard_map/all_to_all | solution.py:45
  29.6 0.3 fusion.27
  29.9 0.4 fusion.15
  30.4 1.6 %copy.22 = bf16[32,64,128]{1,0,2:T(8,128)(2,1)S(1)} copy(bf16[32,64,128]{2,1,0:T(8,128)(2,1)S(1)} %fusion.15) | data formatting | bytes 1048576 | tf_op jit(solution)/shard_map/convert_element_type | solution.py:25
  32.0 0.7 reshape.30
  32.7 12.1 %all_to_all.46 = bf16[8,2,16384]{2,1,0:T(2,128)(2,1)S(1)} all-to-all(bf16[8,2,16384]{2,1,0:T(2,128)(2,1)S(1)} %reshape.30), channel_id=1, replica_groups=mesh['pr'=8,'pc'=4] {'pr'}, dimensions={0} | all-to-all | bytes 1048576 | tf_op jit(solution)/shard_map/all_to_all | solution.py:46
  44.8 0.7 reshape.31
  45.5 0.4 copy.24
  45.9 28.9 %all-gather.2.cloned.1.call-done = bf16[256,256,16]{0,1,2:T(8,128)(2,1)} async-done(((bf16[256,64,16]{0,1,2:T(8,128)(2,1)}), bf16[256,256,16]{0,1,2:T(8,128)(2,1)}) %all-gather.2.cloned.1.call-update) | async-done | bytes 2097168 | tf_op jit(solution)/shard_map/all_gather | solution.py:50
  74.8 2.4 %fusion.18 = bf16[256,64,16]{0,1,2:T(8,128)(2,1)S(1)} fusion(bf16[256,256,16]{0,1,2:T(8,128)(2,1)} %all-gather.2.cloned.1.call-done, bf16[256,64,16]{1,2,0:T(8,128)(2,1)S(1)} %bitcast.61), kind=kOutput, calls=%fused_computation.26 | convolution fusion | flops 134742016 | bytes 3145728 | tf_op jit(solution)/shard_map/kid,kjd->ijd/dot_general | solution.py:48
  77.2 1.0 copy.30
  78.1 1.5 %reshape.32 = bf16[8,2,16384]{2,1,0:T(2,128)(2,1)} reshape(bf16[256,16,64]{2,1,0:T(8,128)(2,1)S(1)} %bitcast.64) | data formatting | bytes 1048576
  79.6 3.7 %all-to-all-start.2 = ((bf16[8,2,16384]{2,1,0:T(2,128)(2,1)}), bf16[8,2,16384]{2,1,0:T(2,128)(2,1)S(1)}, u32[]{:S(2)}, u32[]{:S(2)}) async-start(bf16[8,2,16384]{2,1,0:T(2,128)(2,1)} %reshape.32), calls=%async_computation.2 | async-start | bytes 1048576 | tf_op jit(solution)/shard_map/all_to_all | solution.py:55
  83.3 0.4 fusion.13
  83.8 9.3 %all-to-all-done.2 = bf16[8,2,16384]{2,1,0:T(2,128)(2,1)S(1)} async-done(((bf16[8,2,16384]{2,1,0:T(2,128)(2,1)}), bf16[8,2,16384]{2,1,0:T(2,128)(2,1)S(1)}, u32[]{:S(2)}, u32[]{:S(2)}) %all-to-all-start.2) | async-done | bytes 524320 | tf_op jit(solution)/shard_map/all_to_all | solution.py:55
  93.0 0.7 reshape.33
  93.7 0.2 convert_bitcast_fusion
  93.9 0.2 fusion.19
  94.1 0.4 multiply_reduce_fusion
  94.5 0.3 copy.31
  94.8 0.4 copy-done.3
  95.2 0.5 fusion.2
  95.6 0.3 copy-done.2
  95.9 1.3 %fusion.17 = bf16[32,64,128]{2,1,0:T(8,128)(2,1)} fusion(f32[32,64,128]{2,1,0:T(8,128)S(1)} %fusion.13, bf16[32,64,128]{1,2,0:T(8,128)(2,1)S(1)} %fusion.2, bf16[128,128]{1,0:T(8,128)(2,1)S(1)} %copy-done.2), kind=kOutput, calls=%fused_computation.25 | convolution fusion | flops 67633152 | bytes 2129920 | tf_op jit(solution)/shard_map/ijd,dc->ijc/dot_general | solution.py:35
  (13 shorter events, 0.1 us)
Async XLA Ops:
  6.5 1.0 %copy-start = (bf16[32,64,128]{2,1,0:T(8,128)(2,1)S(1)}, bf16[32,64,128]{2,1,0:T(8,128)(2,1)}, u32[]{:S(2)}) copy-start(bf16[32,64,128]{2,1,0:T(8,128)(2,1)} %param.8) | copy-start | bytes 1572868
  6.5 68.3 %all-gather.2.cloned.1.call-start = ((), (), s32[]{:S(2)}) async-start(), calls=%async_computation.3 | async-start | bytes 2621440 | tf_op jit(solution)/shard_map/all_gather | solution.py:50
  27.5 2.1 %copy-start.1 = (bf16[128,128]{1,0:T(8,128)(2,1)S(1)}, bf16[128,128]{1,0:T(8,128)(2,1)}, u32[]{:S(2)}) copy-start(bf16[128,128]{1,0:T(8,128)(2,1)} %param.10) | copy-start | bytes 98308
  27.9 2.0 %copy-start.4 = (bf16[128,128]{1,0:T(8,128)(2,1)S(1)}, bf16[128,128]{1,0:T(8,128)(2,1)}, u32[]{:S(2)}) copy-start(bf16[128,128]{1,0:T(8,128)(2,1)} %param.12) | copy-start | bytes 98308
  77.2 6.2 %copy-start.5 = (bf16[128,128]{1,0:T(8,128)(2,1)S(1)}, bf16[128,128]{1,0:T(8,128)(2,1)}, u32[]{:S(2)}) copy-start(bf16[128,128]{1,0:T(8,128)(2,1)} %param.15) | copy-start | bytes 98308
  79.6 13.4 %all-to-all-start.2 = ((bf16[8,2,16384]{2,1,0:T(2,128)(2,1)}), bf16[8,2,16384]{2,1,0:T(2,128)(2,1)S(1)}, u32[]{:S(2)}, u32[]{:S(2)}) async-start(bf16[8,2,16384]{2,1,0:T(2,128)(2,1)} %reshape.32), calls=%async_computation.2 | async-start | bytes 1048576 | tf_op jit(solution)/shard_map/all_to_all | solution.py:55
  94.5 0.7 copy-start.3
  95.2 0.8 copy-start.2
Sparse Core Ops, SparseCore 0:
  29.7 45.0 all-gather.1
where the time goes:
time: 105 us; the launch traced here: 104 us
  waiting for transfers between devices  38.2 us (36%)
  blocking collectives  26.8 us (26%)
  between operations  13.6 us (13%)
  local copies, waits for them, and re-layouts  13.5 us (13%)
  matrix products  6.96 us (7%)
  starting transfers between devices  3.68 us (4%)
  other arithmetic  1.27 us (1%)
    all_gather x1, waiting for transfers between devices, on_device(): lax.all_gather(left_lines, 'pc', axis=1, tiled=True)  28.9 us
    all_to_all x1, blocking collectives, on_device(): lax.all_to_all(left, 'pr', split_axis=2, concat_axis=0, tiled=True)  14.7 us
    all_to_all x1, blocking collectives, on_device(): lax.all_to_all(right, 'pr', split_axis=2, concat_axis=0, tiled=True)  12.1 us
    all_to_all x1, waiting for transfers between devices, on_device(): mixed = lax.all_to_all(strip, 'pr', split_axis=0, concat_axis=2, tiled=True)  9.25 us
    unnamed x18, local copies, waits for them, and re-layouts  6.59 us
    all_to_all x1, starting transfers between devices, on_device(): mixed = lax.all_to_all(strip, 'pr', split_axis=0, concat_axis=2, tiled=True)  3.67 us
    convert_element_type x2, local copies, waits for them, and re-layouts, make_factors(): return (pair_in, left.astype(jnp.bfloat16), right.astype(jnp.bfloat16))  3.24 us
    dot_general x1, matrix products, on_device(): jnp.einsum('kid,kjd->ijd', lax.all_gather(left_lines, 'pc', axis=1, tiled...  2.35 us
  transfers between devices with their start and end apart: 2, of which 2 were waited for; matrix products, arithmetic and copies ran while one was open for 4% of the time, Pallas kernels for 0%

commit v1 on v0

--- a/solution.py
+++ b/solution.py
@@ -42,7 +42,10 @@
     ready, left, right = make_factors(pair_array, left_weight, right_weight, left_gate, right_gate)
     count = pair_array.shape[0] * lax.axis_size("pr")
     left_lines, right_lines = (
-        lax.all_to_all(left, "pr", split_axis=2, concat_axis=0, tiled=True),
+        jnp.concatenate(
+            lax.all_to_all(jnp.stack(jnp.split(left, lax.axis_size("pr"), axis=2)), "pr", 0, 0),
+            axis=0,
+        ),
         lax.all_to_all(right, "pr", split_axis=2, concat_axis=0, tiled=True),
     )
     strip = jnp.einsum(

time: 105 us -> 117 us (1.11)
  local copies, waits for them, and re-layouts: 13.5 us -> 25.5 us
    another operation x0 -> x10, local copies, waits for them, and re-layouts: none -> 7.74 us  [on_device(): jnp.stack(jnp.split(left, lax.axis_size('pr'), axis=2))]
    unnamed x18 -> x25, local copies, waits for them, and re-layouts: 6.59 us -> 12.8 us
    all_to_all x2 -> x0, local copies, waits for them, and re-layouts: 2.06 us -> none  [on_device(): lax.all_to_all(left, 'pr', split_axis=2, concat_axis=0, tiled=True)]
    reshape x0 -> x1, local copies, waits for them, and re-layouts: none -> 1.65 us  [on_device(): jnp.concatenate(lax.all_to_all(jnp.stack(jnp.split(left, lax.axis_size('p...]
    convert_element_type x2 -> x1, local copies, waits for them, and re-layouts: 3.24 us -> 1.62 us  [make_factors(): return (pair_in, left.astype(jnp.bfloat16), right.astype(jnp.bfloat16))]
where the time goes in v1:
time: 117 us; the launch traced here: 116 us
  waiting for transfers between devices  38.2 us (33%)
  blocking collectives  26.8 us (23%)
  local copies, waits for them, and re-layouts  25.5 us (22%)
  between operations  13.6 us (12%)
  matrix products  6.95 us (6%)
  starting transfers between devices  3.84 us (3%)
  other arithmetic  1.27 us (1%)
    all_gather x1, waiting for transfers between devices, on_device(): lax.all_gather(left_lines, 'pc', axis=1, tiled=True)  28.9 us
    all_to_all x1, blocking collectives, on_device(): lax.all_to_all(jnp.stack(jnp.split(left, lax.axis_size('pr'), axis=2)), '...  14.7 us
    unnamed x25, local copies, waits for them, and re-layouts  12.8 us
    all_to_all x1, blocking collectives, on_device(): lax.all_to_all(right, 'pr', split_axis=2, concat_axis=0, tiled=True)  12.1 us
    all_to_all x1, waiting for transfers between devices, on_device(): mixed = lax.all_to_all(strip, 'pr', split_axis=0, concat_axis=2, tiled=True)  9.28 us
    another operation x10, local copies, waits for them, and re-layouts, on_device(): jnp.stack(jnp.split(left, lax.axis_size('pr'), axis=2))  7.74 us
    all_to_all x1, starting transfers between devices, on_device(): mixed = lax.all_to_all(strip, 'pr', split_axis=0, concat_axis=2, tiled=True)  3.83 us
    dot_general x1, matrix products, on_device(): jnp.einsum('kid,kjd->ijd', lax.all_gather(left_lines, 'pc', axis=1, tiled...  2.35 us
  transfers between devices with their start and end apart: 2, of which 2 were waited for; matrix products, arithmetic and copies ran while one was open for 4% of the time, Pallas kernels for 0%

profile of v1, /device:TPU:0, one launch (start us, length us, event | category | flops | bytes accessed | tf_op | source)
XLA Modules:
  0.0 116.2 jit_solution(363312956391407247)
XLA Ops:
  6.5 1.0 copy-done
  7.6 1.0 fusion.24
  8.6 1.2 %fusion.14 = bf16[32,64,128]{2,1,0:T(8,128)(2,1)S(1)} fusion(f32[32,64,128]{2,1,0:T(8,128)S(1)} %fusion.24, bf16[32,64,128]{2,1,0:T(8,128)(2,1)S(1)} %copy-done, bf16[128,128]{1,0:T(8,128)(2,1)} %param.11), kind=kOutput, calls=%fused_computation.22 | convolution fusion | flops 68419584 | bytes 2129920 | tf_op jit(solution)/shard_map/ijc,cd->ijd/dot_general | solution.py:19
  9.8 2.3 %slice_bitcast_fusion = (bf16[1,32,64,16]{3,2,1,0:T(8,128)(2,1)S(1)}, bf16[1,32,64,16]{3,2,1,0:T(8,128)(2,1)S(1)}, bf16[1,32,64,16]{3,2,1,0:T(8,128)(2,1)S(1)}, ...) fusion(bf16[32,64,128]{2,1,0:T(8,128)(2,1)S(1)} %fusion.14), kind=kLoop, calls=%fused_computation.29 | loop fusion | bytes 1048576 | tf_op jit(solution)/shard_map/stack | solution.py:46
  12.1 1.2 %copy.39 = bf16[1,32,64,16]{2,3,1,0:T(8,128)(2,1)S(1)} copy(bf16[1,32,64,16]{3,2,1,0:T(8,128)(2,1)} %get-tuple-element.12) | data formatting | bytes 131072 | tf_op jit(solution)/shard_map/stack | solution.py:46
  13.4 0.7 constant_dynamic-update-slice_fusion.7
  14.0 1.2 %copy.40 = bf16[1,32,64,16]{2,3,1,0:T(8,128)(2,1)S(1)} copy(bf16[1,32,64,16]{3,2,1,0:T(8,128)(2,1)} %get-tuple-element.11) | data formatting | bytes 131072 | tf_op jit(solution)/shard_map/stack | solution.py:46
  15.3 1.2 %copy.41 = bf16[1,32,64,16]{2,3,1,0:T(8,128)(2,1)S(1)} copy(bf16[1,32,64,16]{3,2,1,0:T(8,128)(2,1)} %get-tuple-element.10) | data formatting | bytes 131072 | tf_op jit(solution)/shard_map/stack | solution.py:46
  17.6 0.7 constant_dynamic-update-slice_fusion.6
  18.2 0.7 constant_dynamic-update-slice_fusion.5
  18.9 0.7 constant_dynamic-update-slice_fusion.4
  19.6 0.7 constant_dynamic-update-slice_fusion.3
  20.2 0.7 constant_dynamic-update-slice_fusion.2
  20.9 0.7 constant_dynamic-update-slice_fusion.1
  21.5 0.7 constant_dynamic-update-slice_fusion
  22.2 2.3 %reshape.32 = bf16[8,2,16384]{2,1,0:T(2,128)(2,1)S(1)} reshape(bf16[8,32,16,64]{3,2,1,0:T(8,128)(2,1)} %bitcast.79) | data formatting | bytes 1048576
  24.5 14.7 %all_to_all.32 = bf16[8,2,16384]{2,1,0:T(2,128)(2,1)S(1)} all-to-all(bf16[8,2,16384]{2,1,0:T(2,128)(2,1)S(1)} %reshape.32), channel_id=1, replica_groups=mesh['pr'=8,'pc'=4] {'pr'}, dimensions={0} | all-to-all | bytes 1048576 | tf_op jit(solution)/shard_map/all_to_all | solution.py:46
  39.2 0.7 reshape.33
  39.9 1.6 %copy.47 = bf16[256,64,16]{0,1,2:T(8,128)(2,1)} copy(bf16[256,64,16]{1,2,0:T(8,128)(2,1)S(1)} %bitcast.75) | data formatting | bytes 1048576 | tf_op jit(solution)/shard_map/reshape | solution.py:45
  42.3 1.6 %copy.36 = bf16[32,64,128]{1,0,2:T(8,128)(2,1)S(1)} copy(bf16[32,64,128]{2,1,0:T(8,128)(2,1)S(1)} %fusion.15) | data formatting | bytes 1048576 | tf_op jit(solution)/shard_map/convert_element_type | solution.py:25
  43.9 0.7 reshape.34
  44.6 12.1 %all_to_all.33 = bf16[8,2,16384]{2,1,0:T(2,128)(2,1)S(1)} all-to-all(bf16[8,2,16384]{2,1,0:T(2,128)(2,1)S(1)} %reshape.34), channel_id=1, replica_groups=mesh['pr'=8,'pc'=4] {'pr'}, dimensions={0} | all-to-all | bytes 1048576 | tf_op jit(solution)/shard_map/all_to_all | solution.py:49
  56.8 0.7 reshape.35
  57.8 28.9 %all-gather.2.cloned.1.call-done = bf16[256,256,16]{0,1,2:T(8,128)(2,1)} async-done(((bf16[256,64,16]{0,1,2:T(8,128)(2,1)}), bf16[256,256,16]{0,1,2:T(8,128)(2,1)}) %all-gather.2.cloned.1.call-update) | async-done | bytes 2097168 | tf_op jit(solution)/shard_map/all_gather | solution.py:53
  86.8 2.4 %fusion.18 = bf16[256,64,16]{0,1,2:T(8,128)(2,1)S(1)} fusion(bf16[256,256,16]{0,1,2:T(8,128)(2,1)} %all-gather.2.cloned.1.call-done, bf16[256,64,16]{1,2,0:T(8,128)(2,1)S(1)} %bitcast.74), kind=kOutput, calls=%fused_computation.26 | convolution fusion | flops 134742016 | bytes 3145728 | tf_op jit(solution)/shard_map/kid,kjd->ijd/dot_general | solution.py:51
  89.1 1.0 copy.49
  90.1 1.5 %reshape.36 = bf16[8,2,16384]{2,1,0:T(2,128)(2,1)} reshape(bf16[256,16,64]{2,1,0:T(8,128)(2,1)S(1)} %bitcast.77) | data formatting | bytes 1048576
  91.6 3.8 %all-to-all-start.2 = ((bf16[8,2,16384]{2,1,0:T(2,128)(2,1)}), bf16[8,2,16384]{2,1,0:T(2,128)(2,1)S(1)}, u32[]{:S(2)}, u32[]{:S(2)}) async-start(bf16[8,2,16384]{2,1,0:T(2,128)(2,1)} %reshape.36), calls=%async_computation.2 | async-start | bytes 1048576 | tf_op jit(solution)/shard_map/all_to_all | solution.py:58
  95.9 9.3 %all-to-all-done.2 = bf16[8,2,16384]{2,1,0:T(2,128)(2,1)S(1)} async-done(((bf16[8,2,16384]{2,1,0:T(2,128)(2,1)}), bf16[8,2,16384]{2,1,0:T(2,128)(2,1)S(1)}, u32[]{:S(2)}, u32[]{:S(2)}) %all-to-all-start.2) | async-done | bytes 524320 | tf_op jit(solution)/shard_map/all_to_all | solution.py:58
  105.1 0.7 reshape.37
  107.3 0.5 fusion.2
  108.1 1.3 %fusion.17 = bf16[32,64,128]{2,1,0:T(8,128)(2,1)} fusion(f32[32,64,128]{2,1,0:T(8,128)S(1)} %fusion.13, bf16[32,64,128]{1,2,0:T(8,128)(2,1)S(1)} %fusion.2, bf16[128,128]{1,0:T(8,128)(2,1)S(1)} %copy-done.2), kind=kOutput, calls=%fused_computation.25 | convolution fusion | flops 67633152 | bytes 2129920 | tf_op jit(solution)/shard_map/ijd,dc->ijc/dot_general | solution.py:35
  (28 shorter events, 4.4 us)
Async XLA Ops:
  6.5 1.0 copy-start
  6.5 80.2 %all-gather.2.cloned.1.call-start = ((), (), s32[]{:S(2)}) async-start(), calls=%async_computation.3 | async-start | bytes 2621440 | tf_op jit(solution)/shard_map/all_gather | solution.py:53
  39.2 2.3 %copy-start.1 = (bf16[128,128]{1,0:T(8,128)(2,1)S(1)}, bf16[128,128]{1,0:T(8,128)(2,1)}, u32[]{:S(2)}) copy-start(bf16[128,128]{1,0:T(8,128)(2,1)} %param.10) | copy-start | bytes 98308
  39.9 2.0 %copy-start.4 = (bf16[128,128]{1,0:T(8,128)(2,1)S(1)}, bf16[128,128]{1,0:T(8,128)(2,1)}, u32[]{:S(2)}) copy-start(bf16[128,128]{1,0:T(8,128)(2,1)} %param.12) | copy-start | bytes 98308
  89.1 6.3 %copy-start.5 = (bf16[128,128]{1,0:T(8,128)(2,1)S(1)}, bf16[128,128]{1,0:T(8,128)(2,1)}, u32[]{:S(2)}) copy-start(bf16[128,128]{1,0:T(8,128)(2,1)} %param.15) | copy-start | bytes 98308
  91.6 13.5 %all-to-all-start.2 = ((bf16[8,2,16384]{2,1,0:T(2,128)(2,1)}), bf16[8,2,16384]{2,1,0:T(2,128)(2,1)S(1)}, u32[]{:S(2)}, u32[]{:S(2)}) async-start(bf16[8,2,16384]{2,1,0:T(2,128)(2,1)} %reshape.36), calls=%async_computation.2 | async-start | bytes 1048576 | tf_op jit(solution)/shard_map/all_to_all | solution.py:58
  106.6 0.7 copy-start.3
  107.3 0.8 copy-start.2
Sparse Core Ops, SparseCore 0:
  41.7 45.0 all-gather.1
